TPU v7x, 32 devices: a whole 2x2x4 slice. The times are simulated.
32 devices in a mesh: cache: 4 (over x, core), expert: 8 (over z, y).
Axes of the slice: x: 2, y: 2, z: 4, core: 2. Of those that a mesh axis runs over, the one named last changes fastest.
Arguments:
- queries: bfloat16 [2, 32, 2048], P(None, 'expert'), may hold values from -16 to 16
- k_cache: bfloat16 [32, 4096, 256], P('expert', 'cache'), may hold values from -6 to 6
- v_cache: bfloat16 [32, 4096, 256], P('expert', 'cache'), may hold values from -6 to 6
- lengths: int32 [32], P('expert'), may hold values from 1 to 4094
- w_out: bfloat16 [2048, 2880], P('cache'), may hold values from -0.125 to 0.125
- norm_gain: float32 [2880], replicated, may hold values from 0.25 to 1.75
- w_gate: bfloat16 [8, 2880, 1440], P('cache', 'expert'), may hold values from -0.109375 to 0.109375
- w_up: bfloat16 [8, 2880, 1440], P('cache', 'expert'), may hold values from -0.109375 to 0.109375
- w_down: bfloat16 [8, 1440, 2880], P('cache', None, 'expert'), may hold values from -0.15625 to 0.15625
- expert_ids: int32 [2, 32, 4], P(None, 'expert'), may hold values from 0 to 7, all different within a row; in each aligned block of 4 rows (0 to 3, 4 to 7, ..., all dimensions but the last counted through in order) at most 2 rows name the same one
- gate_weights: float32 [2, 32, 4], P(None, 'expert'), may hold values from 0.1 to 1
Outputs:
- mixed: bfloat16 [2, 32, 2880], P(None, 'expert')
- gate_owner: bfloat16 [8, 2880, 1440], P('expert', None, 'cache')
- up_owner: bfloat16 [8, 2880, 1440], P('expert', None, 'cache')
- down_owner: bfloat16 [8, 1440, 2880], P('expert', 'cache')
Inputs may be any that keep to these rules, and one draw needn't show every extreme that they name: `expert_ids`: in each step the 4 rows of one index of expert name one expert at most 2 times; a row names 4 different experts.
All inputs are finite; a program needn't handle non-finite values.
Results may differ from a plain program's by a relative error of at most 0.015.
Values may be sent and summed in bfloat16 or wider, within the bound.
A program may use at most 64 MiB of HBM per device.

v0:
```python
import math
import jax
import jax.numpy as jnp
from jax import lax
from jax.sharding import PartitionSpec as P

D = 2880
QH = 32
KVH = 4
HD = 64
TOP = 4


def joined(part, axis, combine):
    gathered = jax.tree.map(lambda a: lax.all_gather(a, axis), part)

    def take(source):
        return jax.tree.map(lambda a: lax.dynamic_index_in_dim(a, source, 0, False), gathered)

    return lax.fori_loop(
        1, lax.axis_size(axis), lambda source, state: combine(state, take(source)), take(0)
    )


def merge_partials(first, second):
    first_high, first_mass, first_accum = first
    second_high, second_mass, second_accum = second
    shared = jnp.maximum(first_high, second_high)
    first_factor = jnp.exp(first_high - shared)
    second_factor = jnp.exp(second_high - shared)
    head_width = first_accum.shape[-1] // first_high.shape[-1]
    accum = first_accum * jnp.repeat(first_factor, head_width, axis=-1) + second_accum * jnp.repeat(
        second_factor, head_width, axis=-1
    )
    return (shared, first_mass * first_factor + second_mass * second_factor, accum)


def shards(
    queries,
    k_cache,
    v_cache,
    lengths,
    w_out,
    norm_gain,
    w_gate,
    w_up,
    w_down,
    expert_ids,
    gate_weights,
):
    gate_owner, up_owner = (
        lax.all_to_all(
            lax.all_to_all(w_gate, "cache", split_axis=2, concat_axis=0, tiled=True),
            "expert",
            split_axis=0,
            concat_axis=1,
            tiled=True,
        ),
        lax.all_to_all(
            lax.all_to_all(w_up, "cache", split_axis=2, concat_axis=0, tiled=True),
            "expert",
            split_axis=0,
            concat_axis=1,
            tiled=True,
        ),
    )
    down_owner = lax.all_to_all(
        lax.all_to_all(w_down, "cache", split_axis=1, concat_axis=0, tiled=True),
        "expert",
        split_axis=0,
        concat_axis=2,
        tiled=True,
    )
    cache_count = lax.axis_size("cache")
    cache_place = lax.axis_index("cache")
    step_count = queries.shape[0]
    row_count = k_cache.shape[0]
    positions = k_cache.shape[1]
    group_size = QH // KVH
    query_heads = queries.reshape(step_count, row_count, KVH, group_size, HD)
    key_heads = k_cache.reshape(row_count, positions, KVH, HD)
    value_heads = v_cache.reshape(row_count, positions, KVH, HD)
    scores = jnp.einsum(
        "srhgd,rphd->srhgp", query_heads, key_heads, preferred_element_type=jnp.float32
    ) * (1.0 / math.sqrt(HD))
    position = cache_place * positions + jnp.arange(positions, dtype=jnp.int32)
    limit = lengths[None, :] + jnp.arange(step_count, dtype=jnp.int32)[:, None] + 1
    visible = (position[None, None, :] < limit[:, :, None])[:, :, None, None, :]
    highest = jnp.max(jnp.where(visible, scores, -1e30), axis=-1)
    weights = jnp.where(visible, jnp.exp(scores - highest[..., None]), 0.0)
    mass = jnp.sum(weights, axis=-1).reshape(step_count, row_count, QH)
    accum = jnp.einsum(
        "srhgp,rphd->srhgd",
        weights.astype(jnp.bfloat16),
        value_heads,
        preferred_element_type=jnp.float32,
    )
    accum = accum.reshape(step_count, row_count, QH * HD)
    highest = highest.reshape(step_count, row_count, QH)
    own_width = w_out.shape[0]
    all_high, all_mass, all_accum = joined((highest, mass, accum), "cache", merge_partials)
    heads_out = all_accum / jnp.repeat(all_mass, HD, axis=-1)
    own_out = lax.dynamic_slice_in_dim(heads_out, cache_place * own_width, own_width, 2)
    own_rows = own_out.astype(jnp.bfloat16).reshape(step_count * row_count, own_width)
    projected = jnp.dot(own_rows, w_out, preferred_element_type=jnp.float32)
    attention = lax.psum(projected, "cache")
    scale = lax.rsqrt(jnp.mean(attention * attention, axis=-1, keepdims=True) + 1e-05)
    normed = (attention * scale * norm_gain).astype(jnp.bfloat16).reshape(step_count, row_count, D)
    experts_total = w_gate.shape[0] * cache_count
    capacity = max(2, (row_count * TOP + experts_total - 1) // experts_total)
    expert_range = jnp.arange(experts_total, dtype=jnp.int32)
    onehot = (expert_ids[..., None] == expert_range).astype(jnp.float32)
    chosen = jnp.sum(onehot, axis=2)
    gate_map = jnp.sum(onehot * gate_weights[..., None], axis=2)
    earlier = jnp.tril(jnp.ones((row_count, row_count), jnp.float32), -1)
    ranks = jnp.einsum("rq,sqe->sre", earlier, chosen, precision=lax.Precision.HIGHEST)
    slot_table = (ranks[..., None] == jnp.arange(capacity, dtype=jnp.float32)).astype(
        jnp.float32
    ) * chosen[..., None]
    outgoing = jnp.einsum(
        "srec,srd->escd",
        slot_table.astype(jnp.bfloat16),
        normed,
        preferred_element_type=jnp.float32,
    )
    outgoing = outgoing.astype(jnp.bfloat16).reshape(experts_total, step_count * capacity, D)
    slots = lax.all_to_all(outgoing, "expert", split_axis=0, concat_axis=0, tiled=True)
    source_count = slots.shape[0]
    item_count = slots.shape[1]
    slot_rows = slots.reshape(source_count * item_count, D)
    gate_value = jnp.dot(slot_rows, gate_owner[0], preferred_element_type=jnp.float32)
    up_value = jnp.dot(slot_rows, up_owner[0], preferred_element_type=jnp.float32)
    hidden = (jax.nn.silu(gate_value) * up_value).astype(jnp.bfloat16)
    partial_out = jnp.dot(hidden, down_owner[0], preferred_element_type=jnp.float32).reshape(
        source_count, item_count, D
    )
    expert_out = lax.psum(partial_out, "cache").astype(jnp.bfloat16)
    returned = lax.all_to_all(expert_out, "expert", split_axis=0, concat_axis=0, tiled=True)
    back_width = returned.shape[-1]
    returned = returned.reshape(experts_total, step_count, capacity, back_width)
    combined = jnp.einsum(
        "srec,escd->srd",
        slot_table * gate_map[..., None],
        returned.astype(jnp.float32),
        precision=lax.Precision.HIGHEST,
    )
    attention_rows = attention.reshape(step_count, row_count, D)
    mixed = (attention_rows + combined).astype(jnp.bfloat16)
    return (mixed, gate_owner, up_owner, down_owner)


def solution(mesh):
    return jax.shard_map(
        shards,
        mesh=mesh,
        in_specs=(
            P(None, "expert", None),
            P("expert", "cache", None),
            P("expert", "cache", None),
            P("expert"),
            P("cache", None),
            P(),
            P("cache", "expert", None),
            P("cache", "expert", None),
            P("cache", None, "expert"),
            P(None, "expert", None),
            P(None, "expert", None),
        ),
        out_specs=(
            P(None, "expert", None),
            P("expert", None, "cache"),
            P("expert", None, "cache"),
            P("expert", "cache", None),
        ),
        check_vma=False,
    )
```

profile of v0, /device:TPU:0, one launch (start us, length us, event | category | flops | bytes accessed | tf_op | source)
XLA Modules:
  0.0 412.6 jit_solution(15657608075601051097)
XLA Ops:
  16.5 6.7 %all_gather.10 = f32[4,2,4,32]{3,2,1,0:T(4,128)} all-gather(f32[1,2,4,32]{3,2,1,0:T(4,128)S(1)} %all_gather_reshape.10), channel_id=1, replica_groups=mesh['cache'=4,'expert'=8] {'cache'}, dimensions={0}, use_global_device_ids=true | all-gather | bytes 5120 | tf_op jit(solution)/shard_map/all_gather | solution.py:15
  24.0 5.8 %all_gather.9 = f32[4,2,4,32]{3,2,1,0:T(4,128)} all-gather(f32[1,2,4,32]{3,2,1,0:T(4,128)S(1)} %all_gather_reshape.9), channel_id=1, replica_groups=mesh['cache'=4,'expert'=8] {'cache'}, dimensions={0}, use_global_device_ids=true | all-gather | bytes 5120 | tf_op jit(solution)/shard_map/all_gather | solution.py:15
  37.2 6.0 %all_gather.11 = f32[4,2,4,2048]{3,2,1,0:T(4,128)S(1)} all-gather(f32[1,2,4,2048]{3,2,1,0:T(4,128)S(1)} %all_gather_reshape.11), channel_id=1, replica_groups=mesh['cache'=4,'expert'=8] {'cache'}, dimensions={0}, use_global_device_ids=true | all-gather | bytes 327680 | tf_op jit(solution)/shard_map/all_gather | solution.py:15
  48.9 32.8 %all-reduce.3.cloned.1.call-done = f32[8,2880]{1,0:T(8,128)} async-done(((f32[8,2880]{1,0:T(8,128)}), f32[8,2880]{1,0:T(8,128)}) %all-reduce.3.cloned.1.call-update) | async-done | bytes 92176 | tf_op jit(solution)/shard_map/psum | solution.py:106
  84.8 5.5 %all-to-all-start = ((bf16[8,4,2880]{2,1,0:T(4,128)(2,1)}), bf16[8,4,2880]{2,1,0:T(4,128)(2,1)S(1)}, u32[]{:S(2)}, u32[]{:S(2)}) async-start(bf16[8,4,2880]{2,1,0:T(4,128)(2,1)} %copy.80), calls=%async_computation | async-start | bytes 376832 | tf_op jit(solution)/shard_map/all_to_all | solution.py:127
  90.3 6.8 %copy.81 = bf16[2,360,1440]{1,0,2:T(2,128)(2,1)} copy(bf16[2,360,1440]{2,1,0:T(8,128)(2,1)} %param.19) | data formatting | bytes 4147200 | tf_op args[6]
  98.0 4.5 %all-to-all-start.1 = ((bf16[2,360,1440]{1,0,2:T(2,128)(2,1)}), bf16[2,360,1440]{1,0,2:T(2,128)(2,1)}, u32[]{:S(2)}, u32[]{:S(2)}) async-start(bf16[2,360,1440]{1,0,2:T(2,128)(2,1)} %copy.81), calls=%async_computation.1 | async-start | bytes 4423680 | tf_op jit(solution)/shard_map/all_to_all | solution.py:53
  102.5 6.8 %copy.84 = bf16[2,360,1440]{1,0,2:T(2,128)(2,1)} copy(bf16[2,360,1440]{2,1,0:T(8,128)(2,1)} %param.20) | data formatting | bytes 4147200 | tf_op args[7]
  109.3 20.2 %all-to-all-done.1 = bf16[2,360,1440]{1,0,2:T(2,128)(2,1)} async-done(((bf16[2,360,1440]{1,0,2:T(2,128)(2,1)}), bf16[2,360,1440]{1,0,2:T(2,128)(2,1)}, u32[]{:S(2)}, u32[]{:S(2)}) %all-to-all-start.1) | async-done | bytes 2073632 | tf_op jit(solution)/shard_map/all_to_all | solution.py:53
  129.5 4.5 %all-to-all-start.3 = ((bf16[2,360,1440]{1,0,2:T(2,128)(2,1)}), bf16[2,360,1440]{1,0,2:T(2,128)(2,1)}, u32[]{:S(2)}, u32[]{:S(2)}) async-start(bf16[2,360,1440]{1,0,2:T(2,128)(2,1)} %copy.84), calls=%async_computation.3 | async-start | bytes 4423680 | tf_op jit(solution)/shard_map/all_to_all | solution.py:60
  134.0 12.9 %copy.87 = bf16[2,1440,360]{2,0,1:T(2,128)(2,1)} copy(bf16[2,1440,360]{2,1,0:T(8,128)(2,1)} %param.21) | data formatting | bytes 4147200 | tf_op args[8]
  146.9 14.0 %all-to-all-done.3 = bf16[2,360,1440]{1,0,2:T(2,128)(2,1)} async-done(((bf16[2,360,1440]{1,0,2:T(2,128)(2,1)}), bf16[2,360,1440]{1,0,2:T(2,128)(2,1)}, u32[]{:S(2)}, u32[]{:S(2)}) %all-to-all-start.3) | async-done | bytes 2073632 | tf_op jit(solution)/shard_map/all_to_all | solution.py:60
  160.9 4.5 %all-to-all-start.5 = ((bf16[2,1440,360]{2,0,1:T(2,128)(2,1)}), bf16[2,1440,360]{2,0,1:T(2,128)(2,1)}, u32[]{:S(2)}, u32[]{:S(2)}) async-start(bf16[2,1440,360]{2,0,1:T(2,128)(2,1)} %copy.87), calls=%async_computation.5 | async-start | bytes 4423680 | tf_op jit(solution)/shard_map/all_to_all | solution.py:68
  168.7 23.6 %all-to-all-done.5 = bf16[2,1440,360]{2,0,1:T(2,128)(2,1)} async-done(((bf16[2,1440,360]{2,0,1:T(2,128)(2,1)}), bf16[2,1440,360]{2,0,1:T(2,128)(2,1)}, u32[]{:S(2)}, u32[]{:S(2)}) %all-to-all-start.5) | async-done | bytes 2073632 | tf_op jit(solution)/shard_map/all_to_all | solution.py:68
  192.3 5.1 %all-to-all-start.2 = ((bf16[8,360,360]{1,2,0:T(8,128)(2,1)}), bf16[8,360,360]{1,2,0:T(8,128)(2,1)}, u32[]{:S(2)}, u32[]{:S(2)}) async-start(bf16[8,360,360]{1,2,0:T(8,128)(2,1)} %bitcast.104), calls=%async_computation.2 | async-start | bytes 4423680 | tf_op jit(solution)/shard_map/all_to_all | solution.py:52
  200.8 47.1 %all-to-all-done.2 = bf16[8,360,360]{1,2,0:T(8,128)(2,1)} async-done(((bf16[8,360,360]{1,2,0:T(8,128)(2,1)}), bf16[8,360,360]{1,2,0:T(8,128)(2,1)}, u32[]{:S(2)}, u32[]{:S(2)}) %all-to-all-start.2) | async-done | bytes 2073632 | tf_op jit(solution)/shard_map/all_to_all | solution.py:52
  247.9 4.4 %all-to-all-start.4 = ((bf16[8,360,360]{1,2,0:T(8,128)(2,1)}), bf16[8,360,360]{1,2,0:T(8,128)(2,1)}, u32[]{:S(2)}, u32[]{:S(2)}) async-start(bf16[8,360,360]{1,2,0:T(8,128)(2,1)} %bitcast.105), calls=%async_computation.4 | async-start | bytes 4423680 | tf_op jit(solution)/shard_map/all_to_all | solution.py:59
  255.6 46.9 %all-to-all-done.4 = bf16[8,360,360]{1,2,0:T(8,128)(2,1)} async-done(((bf16[8,360,360]{1,2,0:T(8,128)(2,1)}), bf16[8,360,360]{1,2,0:T(8,128)(2,1)}, u32[]{:S(2)}, u32[]{:S(2)}) %all-to-all-start.4) | async-done | bytes 2073632 | tf_op jit(solution)/shard_map/all_to_all | solution.py:59
  302.6 4.5 %all-to-all-start.6 = ((bf16[8,360,360]{2,1,0:T(8,128)(2,1)}), bf16[8,360,360]{2,1,0:T(8,128)(2,1)}, u32[]{:S(2)}, u32[]{:S(2)}) async-start(bf16[8,360,360]{2,1,0:T(8,128)(2,1)} %bitcast.103), calls=%async_computation.6 | async-start | bytes 4423680 | tf_op jit(solution)/shard_map/all_to_all | solution.py:67
  311.4 4.2 %copy.86 = bf16[8,360,360]{2,1,0:T(8,128)(2,1)} copy(bf16[8,360,360]{1,2,0:T(8,128)(2,1)} %all-to-all-done.4) | data formatting | bytes 4147200 | tf_op jit(solution)/shard_map/all_to_all | solution.py:59
  318.4 38.9 %all-to-all-done.6 = bf16[8,360,360]{2,1,0:T(8,128)(2,1)} async-done(((bf16[8,360,360]{2,1,0:T(8,128)(2,1)}), bf16[8,360,360]{2,1,0:T(8,128)(2,1)}, u32[]{:S(2)}, u32[]{:S(2)}) %all-to-all-start.6) | async-done | bytes 2073632 | tf_op jit(solution)/shard_map/all_to_all | solution.py:67
  360.6 4.8 %reshape.124 = bf16[360,2880,1]{1,0,2:T(8,128)(2,1)} reshape(bf16[1,360,8,360]{3,2,1,0:T(8,128)(2,1)} %copy.89) | data formatting | bytes 4147200 | tf_op jit(solution)/shard_map/squeeze | solution.py:134
  367.5 14.8 %all-reduce.4 = bf16[8,4,2880]{2,0,1:T(8,128)(2,1)} all-reduce(f32[8,4,2880]{2,0,1:T(8,128)S(1)} %fusion.15), channel_id=1, replica_groups=mesh['cache'=4,'expert'=8] {'cache'}, use_global_device_ids=true, to_apply=%region_8.9 | all-reduce | flops 92160 | bytes 552960 | tf_op jit(solution)/shard_map/psum | solution.py:137
  383.9 4.3 %all-to-all-start.7 = ((bf16[8,4,2880]{2,1,0:T(4,128)(2,1)}), bf16[8,4,2880]{2,1,0:T(4,128)(2,1)S(1)}, u32[]{:S(2)}, u32[]{:S(2)}) async-start(bf16[8,4,2880]{2,1,0:T(4,128)(2,1)} %copy.91), calls=%async_computation.7 | async-start | bytes 376832 | tf_op jit(solution)/shard_map/all_to_all | solution.py:138
  (87 shorter events, 72.1 us)
Async XLA Ops:
  7.2 39.9 %copy-start = (bf16[512,2880]{0,1:T(8,128)(2,1)S(1)}, bf16[512,2880]{0,1:T(8,128)(2,1)}, u32[]{:S(2)}) copy-start(bf16[512,2880]{0,1:T(8,128)(2,1)} %param.17) | copy-start | bytes 8847364
  7.2 74.6 %all-reduce.3.cloned.1.call-start = ((), (), s32[]{:S(2)}) async-start(), calls=%async_computation.8 | async-start | bytes 188416 | tf_op jit(solution)/shard_map/psum | solution.py:106
  15.1 1.0 copy-start.2
  46.7 1.8 copy-start.5
  46.7 1.8 copy-start.6
  46.8 36.0 %copy-start.4 = (f32[2880]{0:T(1024)S(1)}, f32[2880]{0:T(1024)}, u32[]{:S(2)}) copy-start(f32[2880]{0:T(1024)} %param.18) | copy-start | bytes 34564
  84.8 13.2 %all-to-all-start = ((bf16[8,4,2880]{2,1,0:T(4,128)(2,1)}), bf16[8,4,2880]{2,1,0:T(4,128)(2,1)S(1)}, u32[]{:S(2)}, u32[]{:S(2)}) async-start(bf16[8,4,2880]{2,1,0:T(4,128)(2,1)} %copy.80), calls=%async_computation | async-start | bytes 376832 | tf_op jit(solution)/shard_map/all_to_all | solution.py:127
  98.0 31.4 %all-to-all-start.1 = ((bf16[2,360,1440]{1,0,2:T(2,128)(2,1)}), bf16[2,360,1440]{1,0,2:T(2,128)(2,1)}, u32[]{:S(2)}, u32[]{:S(2)}) async-start(bf16[2,360,1440]{1,0,2:T(2,128)(2,1)} %copy.81), calls=%async_computation.1 | async-start | bytes 4423680 | tf_op jit(solution)/shard_map/all_to_all | solution.py:53
  129.5 31.4 %all-to-all-start.3 = ((bf16[2,360,1440]{1,0,2:T(2,128)(2,1)}), bf16[2,360,1440]{1,0,2:T(2,128)(2,1)}, u32[]{:S(2)}, u32[]{:S(2)}) async-start(bf16[2,360,1440]{1,0,2:T(2,128)(2,1)} %copy.84), calls=%async_computation.3 | async-start | bytes 4423680 | tf_op jit(solution)/shard_map/all_to_all | solution.py:60
  160.9 31.4 %all-to-all-start.5 = ((bf16[2,1440,360]{2,0,1:T(2,128)(2,1)}), bf16[2,1440,360]{2,0,1:T(2,128)(2,1)}, u32[]{:S(2)}, u32[]{:S(2)}) async-start(bf16[2,1440,360]{2,0,1:T(2,128)(2,1)} %copy.87), calls=%async_computation.5 | async-start | bytes 4423680 | tf_op jit(solution)/shard_map/all_to_all | solution.py:68
  192.3 55.6 %all-to-all-start.2 = ((bf16[8,360,360]{1,2,0:T(8,128)(2,1)}), bf16[8,360,360]{1,2,0:T(8,128)(2,1)}, u32[]{:S(2)}, u32[]{:S(2)}) async-start(bf16[8,360,360]{1,2,0:T(8,128)(2,1)} %bitcast.104), calls=%async_computation.2 | async-start | bytes 4423680 | tf_op jit(solution)/shard_map/all_to_all | solution.py:52
  247.9 54.6 %all-to-all-start.4 = ((bf16[8,360,360]{1,2,0:T(8,128)(2,1)}), bf16[8,360,360]{1,2,0:T(8,128)(2,1)}, u32[]{:S(2)}, u32[]{:S(2)}) async-start(bf16[8,360,360]{1,2,0:T(8,128)(2,1)} %bitcast.105), calls=%async_computation.4 | async-start | bytes 4423680 | tf_op jit(solution)/shard_map/all_to_all | solution.py:59
  302.6 54.7 %all-to-all-start.6 = ((bf16[8,360,360]{2,1,0:T(8,128)(2,1)}), bf16[8,360,360]{2,1,0:T(8,128)(2,1)}, u32[]{:S(2)}, u32[]{:S(2)}) async-start(bf16[8,360,360]{2,1,0:T(8,128)(2,1)} %bitcast.103), calls=%async_computation.6 | async-start | bytes 4423680 | tf_op jit(solution)/shard_map/all_to_all | solution.py:67
  315.6 2.3 copy-start.1
  365.4 22.8 %copy-start.3 = (f32[8,2880]{1,0:T(8,128)S(1)}, f32[8,2880]{1,0:T(8,128)}, u32[]{:S(2)}) copy-start(f32[8,2880]{1,0:T(8,128)} %all-reduce.3.cloned.1.call-done) | copy-start | bytes 276484
  383.9 20.9 %all-to-all-start.7 = ((bf16[8,4,2880]{2,1,0:T(4,128)(2,1)}), bf16[8,4,2880]{2,1,0:T(4,128)(2,1)S(1)}, u32[]{:S(2)}, u32[]{:S(2)}) async-start(bf16[8,4,2880]{2,1,0:T(4,128)(2,1)} %copy.91), calls=%async_computation.7 | async-start | bytes 376832 | tf_op jit(solution)/shard_map/all_to_all | solution.py:138
Sparse Core Ops, SparseCore 0:
  48.7 33.0 all-reduce.2
where the time goes:
time: 415 us; the launch traced here: 413 us
  waiting for transfers between devices  225 us (54%)
  local copies, waits for them, and re-layouts  85.2 us (21%)
  starting transfers between devices  37.3 us (9%)
  blocking collectives  33.2 us (8%)
  between operations  14.3 us (3%)
  matrix products  12.3 us (3%)
  other arithmetic  5.74 us (1%)
    unnamed x22, local copies, waits for them, and re-layouts  47.8 us
    all_to_all x1, waiting for transfers between devices, shards(): lax.all_to_all(lax.all_to_all(w_gate, 'cache', split_axis=2, concat_axis=...  47.1 us
    all_to_all x1, waiting for transfers between devices, shards(): lax.all_to_all(lax.all_to_all(w_up, 'cache', split_axis=2, concat_axis=0,...  46.9 us
    all_to_all x1, waiting for transfers between devices, shards(): lax.all_to_all(lax.all_to_all(w_down, 'cache', split_axis=1, concat_axis=...  38.9 us
    psum x1, waiting for transfers between devices, shards(): attention = lax.psum(projected, 'cache')  32.8 us
    all_to_all x1, waiting for transfers between devices, shards(): lax.all_to_all(w_down, 'cache', split_axis=1, concat_axis=0, tiled=True)  23.6 us
    all_to_all x1, waiting for transfers between devices, shards(): lax.all_to_all(w_gate, 'cache', split_axis=2, concat_axis=0, tiled=True)  20.2 us
    all_gather x3, blocking collectives, joined(): gathered = jax.tree.map(lambda a: lax.all_gather(a, axis), part)  18.5 us
  transfers between devices with their start and end apart: 9, of which 8 were waited for; matrix products, arithmetic and copies ran while one was open for 16% of the time, Pallas kernels for 0%

commit v1 on v0

--- a/solution.py
+++ b/solution.py
@@ -103,7 +103,7 @@
     own_out = lax.dynamic_slice_in_dim(heads_out, cache_place * own_width, own_width, 2)
     own_rows = own_out.astype(jnp.bfloat16).reshape(step_count * row_count, own_width)
     projected = jnp.dot(own_rows, w_out, preferred_element_type=jnp.float32)
-    attention = lax.psum(projected, "cache")
+    attention = jnp.sum(lax.all_gather(projected, "cache"), axis=0)
     scale = lax.rsqrt(jnp.mean(attention * attention, axis=-1, keepdims=True) + 1e-05)
     normed = (attention * scale * norm_gain).astype(jnp.bfloat16).reshape(step_count, row_count, D)
     experts_total = w_gate.shape[0] * cache_count

time: 415 us -> 369 us (0.89)
  waiting for transfers between devices: 225 us -> 195 us
  between operations: 14.3 us -> 0.9 us
  blocking collectives: 33.2 us -> 39.3 us
  starting transfers between devices: 37.3 us -> 32.9 us
    psum x1 -> x0, waiting for transfers between devices: 32.8 us -> none  [shards(): attention = lax.psum(projected, 'cache')]
    all_gather x0 -> x1, blocking collectives: none -> 6.62 us  [shards(): attention = jnp.sum(lax.all_gather(projected, 'cache'), axis=0)]
    unnamed x22 -> x34, local copies, waits for them, and re-layouts: 47.8 us -> 49.9 us
  transfers between devices with their start and end apart: 9 -> 8, of which waited for: 8 -> 7; matrix products, arithmetic and copies ran while one was open for 16% -> 16% of each run, Pallas kernels for 0% -> 0%
where the time goes in v1:
time: 369 us; the launch traced here: 367 us
  waiting for transfers between devices  195 us (53%)
  local copies, waits for them, and re-layouts  83 us (22%)
  blocking collectives  39.3 us (11%)
  starting transfers between devices  32.9 us (9%)
  matrix products  11.6 us (3%)
  other arithmetic  3.89 us (1%)
    unnamed x34, local copies, waits for them, and re-layouts  49.9 us
    all_to_all x1, waiting for transfers between devices, shards(): lax.all_to_all(lax.all_to_all(w_gate, 'cache', split_axis=2, concat_axis=...  47.4 us
    all_to_all x1, waiting for transfers between devices, shards(): lax.all_to_all(lax.all_to_all(w_up, 'cache', split_axis=2, concat_axis=0,...  46.9 us
    all_to_all x1, waiting for transfers between devices, shards(): lax.all_to_all(lax.all_to_all(w_down, 'cache', split_axis=1, concat_axis=...  39.5 us
    all_to_all x1, waiting for transfers between devices, shards(): lax.all_to_all(w_down, 'cache', split_axis=1, concat_axis=0, tiled=True)  23.5 us
    all_to_all x1, waiting for transfers between devices, shards(): lax.all_to_all(w_gate, 'cache', split_axis=2, concat_axis=0, tiled=True)  20 us
    all_gather x3, blocking collectives, joined(): gathered = jax.tree.map(lambda a: lax.all_gather(a, axis), part)  18.5 us
    psum x1, blocking collectives, shards(): expert_out = lax.psum(partial_out, 'cache').astype(jnp.bfloat16)  14.2 us
  transfers between devices with their start and end apart: 8, of which 7 were waited for; matrix products, arithmetic and copies ran while one was open for 16% of the time, Pallas kernels for 0%

profile of v1, /device:TPU:0, one launch (start us, length us, event | category | flops | bytes accessed | tf_op | source)
XLA Modules:
  0.0 366.7 jit_solution(17586536042549778452)
XLA Ops:
  2.4 4.0 %copy.74 = bf16[4,1024,256]{1,2,0:T(8,128)(2,1)} copy(bf16[4,1024,256]{2,1,0:T(8,128)(2,1)} %param.14) | data formatting | bytes 4194304 | tf_op args[1]
  10.0 6.7 %all_gather.16 = f32[4,2,4,32]{3,2,1,0:T(4,128)} all-gather(f32[1,2,4,32]{3,2,1,0:T(4,128)S(1)} %all_gather_reshape.10), channel_id=1, replica_groups=mesh['cache'=4,'expert'=8] {'cache'}, dimensions={0}, use_global_device_ids=true | all-gather | bytes 5120 | tf_op jit(solution)/shard_map/all_gather | solution.py:15
  17.4 5.8 %all_gather.15 = f32[4,2,4,32]{3,2,1,0:T(4,128)} all-gather(f32[1,2,4,32]{3,2,1,0:T(4,128)S(1)} %all_gather_reshape.9), channel_id=1, replica_groups=mesh['cache'=4,'expert'=8] {'cache'}, dimensions={0}, use_global_device_ids=true | all-gather | bytes 5120 | tf_op jit(solution)/shard_map/all_gather | solution.py:15
  23.9 3.9 %copy.78 = bf16[4,1024,256]{1,2,0:T(8,128)(2,1)} copy(bf16[4,1024,256]{2,1,0:T(8,128)(2,1)} %param.15) | data formatting | bytes 4194304 | tf_op args[2]
  30.6 5.9 %all_gather.17 = f32[4,2,4,2048]{3,2,1,0:T(4,128)S(1)} all-gather(f32[1,2,4,2048]{3,2,1,0:T(4,128)S(1)} %all_gather_reshape.11), channel_id=1, replica_groups=mesh['cache'=4,'expert'=8] {'cache'}, dimensions={0}, use_global_device_ids=true | all-gather | bytes 327680 | tf_op jit(solution)/shard_map/all_gather | solution.py:15
  41.3 6.6 %all-gather = f32[32,2880]{1,0:T(8,128)S(1)} all-gather(f32[8,2880]{1,0:T(8,128)S(1)} %fusion.39), channel_id=2, replica_groups=mesh['cache'=4,'expert'=8] {'cache'}, dimensions={0}, use_global_device_ids=true | all-gather | bytes 460800 | tf_op jit(solution)/shard_map/all_gather | solution.py:106
  49.5 5.9 %all-to-all-start = ((bf16[8,4,2880]{2,1,0:T(4,128)(2,1)}), bf16[8,4,2880]{2,1,0:T(4,128)(2,1)S(1)}, u32[]{:S(2)}, u32[]{:S(2)}) async-start(bf16[8,4,2880]{2,1,0:T(4,128)(2,1)} %copy.80), calls=%async_computation | async-start | bytes 376832 | tf_op jit(solution)/shard_map/all_to_all | solution.py:127
  55.5 4.6 %copy.81 = bf16[2,360,1440]{1,0,2:T(2,128)(2,1)} copy(bf16[2,360,1440]{2,1,0:T(8,128)(2,1)S(1)} %copy-done.9) | data formatting | bytes 4147200 | tf_op args[6]
  67.5 6.9 %copy.84 = bf16[2,360,1440]{1,0,2:T(2,128)(2,1)} copy(bf16[2,360,1440]{2,1,0:T(8,128)(2,1)} %param.20) | data formatting | bytes 4147200 | tf_op args[7]
  74.3 20.0 %all-to-all-done.1 = bf16[2,360,1440]{1,0,2:T(2,128)(2,1)S(1)} async-done(((bf16[2,360,1440]{1,0,2:T(2,128)(2,1)}), bf16[2,360,1440]{1,0,2:T(2,128)(2,1)S(1)}, u32[]{:S(2)}, u32[]{:S(2)}) %all-to-all-start.1) | async-done | bytes 2073632 | tf_op jit(solution)/shard_map/all_to_all | solution.py:53
  99.3 12.9 %copy.87 = bf16[2,1440,360]{2,0,1:T(2,128)(2,1)} copy(bf16[2,1440,360]{2,1,0:T(8,128)(2,1)} %param.21) | data formatting | bytes 4147200 | tf_op args[8]
  112.2 13.9 %all-to-all-done.3 = bf16[2,360,1440]{1,0,2:T(2,128)(2,1)S(1)} async-done(((bf16[2,360,1440]{1,0,2:T(2,128)(2,1)}), bf16[2,360,1440]{1,0,2:T(2,128)(2,1)S(1)}, u32[]{:S(2)}, u32[]{:S(2)}) %all-to-all-start.3) | async-done | bytes 2073632 | tf_op jit(solution)/shard_map/all_to_all | solution.py:60
  134.5 23.5 %all-to-all-done.5 = bf16[2,1440,360]{2,0,1:T(2,128)(2,1)S(1)} async-done(((bf16[2,1440,360]{2,0,1:T(2,128)(2,1)}), bf16[2,1440,360]{2,0,1:T(2,128)(2,1)S(1)}, u32[]{:S(2)}, u32[]{:S(2)}) %all-to-all-start.5) | async-done | bytes 2073632 | tf_op jit(solution)/shard_map/all_to_all | solution.py:68
  166.3 47.4 %all-to-all-done.2 = bf16[8,360,360]{1,2,0:T(8,128)(2,1)S(1)} async-done(((bf16[8,360,360]{1,2,0:T(8,128)(2,1)}), bf16[8,360,360]{1,2,0:T(8,128)(2,1)S(1)}, u32[]{:S(2)}, u32[]{:S(2)}) %all-to-all-start.2) | async-done | bytes 2073632 | tf_op jit(solution)/shard_map/all_to_all | solution.py:52
  215.0 4.4 %all-to-all-start.4 = ((bf16[8,360,360]{1,2,0:T(8,128)(2,1)}), bf16[8,360,360]{1,2,0:T(8,128)(2,1)}, u32[]{:S(2)}, u32[]{:S(2)}) async-start(bf16[8,360,360]{1,2,0:T(8,128)(2,1)} %bitcast.114), calls=%async_computation.4 | async-start | bytes 4423680 | tf_op jit(solution)/shard_map/all_to_all | solution.py:59
  222.7 46.9 %all-to-all-done.4 = bf16[8,360,360]{1,2,0:T(8,128)(2,1)} async-done(((bf16[8,360,360]{1,2,0:T(8,128)(2,1)}), bf16[8,360,360]{1,2,0:T(8,128)(2,1)}, u32[]{:S(2)}, u32[]{:S(2)}) %all-to-all-start.4) | async-done | bytes 2073632 | tf_op jit(solution)/shard_map/all_to_all | solution.py:59
  273.5 4.2 %copy.83 = bf16[8,360,360]{2,1,0:T(8,128)(2,1)} copy(bf16[8,360,360]{1,2,0:T(8,128)(2,1)} %copy-done.5) | data formatting | bytes 4147200 | tf_op jit(solution)/shard_map/all_to_all | solution.py:52
  277.7 4.2 %copy.86 = bf16[8,360,360]{2,1,0:T(8,128)(2,1)} copy(bf16[8,360,360]{1,2,0:T(8,128)(2,1)} %all-to-all-done.4) | data formatting | bytes 4147200 | tf_op jit(solution)/shard_map/all_to_all | solution.py:59
  284.7 39.5 %all-to-all-done.6 = bf16[8,360,360]{2,1,0:T(8,128)(2,1)S(1)} async-done(((bf16[8,360,360]{2,1,0:T(8,128)(2,1)}), bf16[8,360,360]{2,1,0:T(8,128)(2,1)S(1)}, u32[]{:S(2)}, u32[]{:S(2)}) %all-to-all-start.6) | async-done | bytes 2073632 | tf_op jit(solution)/shard_map/all_to_all | solution.py:67
  325.9 4.8 %reshape.139 = bf16[360,2880,1]{1,0,2:T(8,128)(2,1)} reshape(bf16[1,360,8,360]{3,2,1,0:T(8,128)(2,1)} %copy.89) | data formatting | bytes 4147200 | tf_op jit(solution)/shard_map/squeeze | solution.py:134
  332.7 14.2 %all-reduce.1 = bf16[8,4,2880]{2,0,1:T(8,128)(2,1)S(1)} all-reduce(f32[8,4,2880]{2,0,1:T(8,128)S(1)} %fusion.18), channel_id=1, replica_groups=mesh['cache'=4,'expert'=8] {'cache'}, use_global_device_ids=true, to_apply=%region_8.9 | all-reduce | flops 92160 | bytes 552960 | tf_op jit(solution)/shard_map/psum | solution.py:137
  347.7 4.4 %all-to-all-start.7 = ((bf16[8,4,2880]{2,1,0:T(4,128)(2,1)}), bf16[8,4,2880]{2,1,0:T(4,128)(2,1)S(1)}, u32[]{:S(2)}, u32[]{:S(2)}) async-start(bf16[8,4,2880]{2,1,0:T(4,128)(2,1)} %copy.91), calls=%async_computation.7 | async-start | bytes 376832 | tf_op jit(solution)/shard_map/all_to_all | solution.py:138
  354.8 4.3 %copy.96 = bf16[1,2880,360]{1,2,0:T(8,128)(2,1)} copy(bf16[1,2880,360]{2,1,0:T(8,128)(2,1)} %bitcast.106) | data formatting | bytes 4147200
  361.5 4.3 %copy.98 = bf16[1,360,2880]{2,1,0:T(8,128)(2,1)} copy(bf16[1,360,2880]{1,2,0:T(8,128)(2,1)} %bitcast.115) | data formatting | bytes 4147200
  (97 shorter events, 70.1 us)
Async XLA Ops:
  0.6 39.8 %copy-start = (bf16[512,2880]{0,1:T(8,128)(2,1)S(1)}, bf16[512,2880]{0,1:T(8,128)(2,1)}, u32[]{:S(2)}) copy-start(bf16[512,2880]{0,1:T(8,128)(2,1)} %param.17) | copy-start | bytes 8847364
  8.6 1.0 copy-start.4
  40.4 7.9 %copy-start.11 = (f32[2,4,4]{2,1,0:T(4,128)S(1)}, f32[2,4,4]{2,1,0:T(4,128)}, u32[]{:S(2)}) copy-start(f32[2,4,4]{2,1,0:T(4,128)} %param.23) | copy-start | bytes 388
  40.4 7.8 %copy-start.12 = (s32[2,4,4]{2,1,0:T(4,128)S(1)}, s32[2,4,4]{2,1,0:T(4,128)}, u32[]{:S(2)}) copy-start(s32[2,4,4]{2,1,0:T(4,128)} %param.22) | copy-start | bytes 388
  40.4 8.1 %copy-start.10 = (f32[2880]{0:T(1024)S(1)}, f32[2880]{0:T(1024)}, u32[]{:S(2)}) copy-start(f32[2880]{0:T(1024)} %param.18) | copy-start | bytes 34564
  41.3 14.2 %copy-start.9 = (bf16[2,360,1440]{2,1,0:T(8,128)(2,1)S(1)}, bf16[2,360,1440]{2,1,0:T(8,128)(2,1)}, u32[]{:S(2)}) copy-start(bf16[2,360,1440]{2,1,0:T(8,128)(2,1)} %param.19) | copy-start | bytes 6220804
  49.5 14.3 %all-to-all-start = ((bf16[8,4,2880]{2,1,0:T(4,128)(2,1)}), bf16[8,4,2880]{2,1,0:T(4,128)(2,1)S(1)}, u32[]{:S(2)}, u32[]{:S(2)}) async-start(bf16[8,4,2880]{2,1,0:T(4,128)(2,1)} %copy.80), calls=%async_computation | async-start | bytes 376832 | tf_op jit(solution)/shard_map/all_to_all | solution.py:127
  63.8 30.5 %all-to-all-start.1 = ((bf16[2,360,1440]{1,0,2:T(2,128)(2,1)}), bf16[2,360,1440]{1,0,2:T(2,128)(2,1)S(1)}, u32[]{:S(2)}, u32[]{:S(2)}) async-start(bf16[2,360,1440]{1,0,2:T(2,128)(2,1)} %copy.81), calls=%async_computation.1 | async-start | bytes 4423680 | tf_op jit(solution)/shard_map/all_to_all | solution.py:53
  94.3 1.3 copy-start.8
  95.7 30.5 %all-to-all-start.3 = ((bf16[2,360,1440]{1,0,2:T(2,128)(2,1)}), bf16[2,360,1440]{1,0,2:T(2,128)(2,1)S(1)}, u32[]{:S(2)}, u32[]{:S(2)}) async-start(bf16[2,360,1440]{1,0,2:T(2,128)(2,1)} %copy.84), calls=%async_computation.3 | async-start | bytes 4423680 | tf_op jit(solution)/shard_map/all_to_all | solution.py:60
  126.1 1.4 copy-start.7
  127.6 30.5 %all-to-all-start.5 = ((bf16[2,1440,360]{2,0,1:T(2,128)(2,1)}), bf16[2,1440,360]{2,0,1:T(2,128)(2,1)S(1)}, u32[]{:S(2)}, u32[]{:S(2)}) async-start(bf16[2,1440,360]{2,0,1:T(2,128)(2,1)} %copy.87), calls=%async_computation.5 | async-start | bytes 4423680 | tf_op jit(solution)/shard_map/all_to_all | solution.py:68
  158.0 1.4 copy-start.6
  159.4 54.2 %all-to-all-start.2 = ((bf16[8,360,360]{1,2,0:T(8,128)(2,1)}), bf16[8,360,360]{1,2,0:T(8,128)(2,1)S(1)}, u32[]{:S(2)}, u32[]{:S(2)}) async-start(bf16[8,360,360]{1,2,0:T(8,128)(2,1)} %bitcast.113), calls=%async_computation.2 | async-start | bytes 4423680 | tf_op jit(solution)/shard_map/all_to_all | solution.py:52
  213.6 1.4 copy-start.5
  215.0 54.6 %all-to-all-start.4 = ((bf16[8,360,360]{1,2,0:T(8,128)(2,1)}), bf16[8,360,360]{1,2,0:T(8,128)(2,1)}, u32[]{:S(2)}, u32[]{:S(2)}) async-start(bf16[8,360,360]{1,2,0:T(8,128)(2,1)} %bitcast.114), calls=%async_computation.4 | async-start | bytes 4423680 | tf_op jit(solution)/shard_map/all_to_all | solution.py:59
  269.6 54.6 %all-to-all-start.6 = ((bf16[8,360,360]{2,1,0:T(8,128)(2,1)}), bf16[8,360,360]{2,1,0:T(8,128)(2,1)S(1)}, u32[]{:S(2)}, u32[]{:S(2)}) async-start(bf16[8,360,360]{2,1,0:T(8,128)(2,1)} %bitcast.112), calls=%async_computation.6 | async-start | bytes 4423680 | tf_op jit(solution)/shard_map/all_to_all | solution.py:67
  281.9 2.3 copy-start.2
  347.7 18.1 %all-to-all-start.7 = ((bf16[8,4,2880]{2,1,0:T(4,128)(2,1)}), bf16[8,4,2880]{2,1,0:T(4,128)(2,1)S(1)}, u32[]{:S(2)}, u32[]{:S(2)}) async-start(bf16[8,4,2880]{2,1,0:T(4,128)(2,1)} %copy.91), calls=%async_computation.7 | async-start | bytes 376832 | tf_op jit(solution)/shard_map/all_to_all | solution.py:138
  354.8 4.3 %copy-start.3 = (bf16[8,360,360]{2,1,0:T(8,128)(2,1)S(1)}, bf16[8,360,360]{2,1,0:T(8,128)(2,1)}, u32[]{:S(2)}) copy-start(bf16[8,360,360]{2,1,0:T(8,128)(2,1)} %copy.86) | copy-start | bytes 6220804
  361.5 5.2 %copy-start.1 = (bf16[512,2880]{0,1:T(8,128)(2,1)S(1)}, bf16[512,2880]{0,1:T(8,128)(2,1)}, u32[]{:S(2)}) copy-start(bf16[512,2880]{0,1:T(8,128)(2,1)} %param.17) | copy-start | bytes 8847364
